TPU v7x, 128 devices: a whole 4x4x4 slice. The times are simulated.
128 devices in a mesh: gx: 8 (over x_lo, z), gy: 4 (over y), gz: 4 (over x_hi, core).
Axes of the slice: x: 4 (x_hi: 2, x_lo: 2; x = x_hi * 2 + x_lo), y: 4, z: 4, core: 2. Of those that a mesh axis runs over, the one named last changes fastest.
Arguments:
- inputs: bfloat16 [2560, 8192], P(('gx', 'gz'), 'gy'), may hold values from -6 to 6
- out_grad: bfloat16 [2560, 8192], P(('gx', 'gz'), 'gy'), may hold values from -6 to 6
- gate_weight: bfloat16 [8192, 16384], P('gy', ('gx', 'gz')), may hold values from -0.0625 to 0.0625
- up_weight: bfloat16 [8192, 16384], P('gy', ('gx', 'gz')), may hold values from -0.0625 to 0.0625
- down_weight: bfloat16 [16384, 8192], P(('gx', 'gz'), 'gy'), may hold values from -0.046875 to 0.046875
Outputs:
- in_grad: bfloat16 [2560, 8192], P(('gx', 'gz'), 'gy')
All inputs are finite; a program needn't handle non-finite values.
Results may differ from a plain program's by a relative error of at most 0.0049.
Values may be sent and summed in bfloat16 or wider, within the bound.
A program may use at most 128 MiB of HBM per device.

v0:
```python
import jax
import jax.numpy as jnp
from jax import lax
from jax.sharding import PartitionSpec as P


def side_by_side(arrays, axis, dim, along):
    widths = [a.shape[along] for a in arrays]
    both = jnp.concatenate(arrays, axis=along)
    filled = lax.all_gather(both, axis, axis=dim, tiled=True)
    return tuple(jnp.split(filled, [sum(widths[:k]) for k in range(1, len(widths))], axis=along))


def side_by_side_2(arrays, axis, dim, along):
    both = jnp.concatenate(arrays, axis=along)
    filled, at, gathered = (lax.psum_scatter(both, axis, scatter_dimension=dim, tiled=True), 0, [])
    for a in arrays:
        gathered.append(lax.slice_in_dim(filled, at, at + a.shape[along], axis=along))
        at += a.shape[along]
    return tuple(gathered)


def contract_last(left, right):
    return lax.dot_general(
        left, right, (((1,), (1,)), ((), ())), preferred_element_type=jnp.float32
    )


def partial_terms(rows_in, rows_grad, gate_cols, up_cols, down_cols):
    gate = jnp.dot(rows_in, gate_cols, preferred_element_type=jnp.float32)
    upper = jnp.dot(rows_in, up_cols, preferred_element_type=jnp.float32)
    hidden_grad = contract_last(rows_grad, down_cols)
    return (gate, upper, hidden_grad)


def local_grads(gate, upper, hidden_grad):
    logistic = jax.nn.sigmoid(gate)
    gate_grad = (hidden_grad * upper * logistic * (1.0 + gate * (1.0 - logistic))).astype(
        jnp.bfloat16
    )
    up_grad = (hidden_grad * gate * logistic).astype(jnp.bfloat16)
    return (gate_grad, up_grad)


def shards(inputs, out_grad, gate_weight, up_weight, down_weight):
    rows_in, rows_grad = side_by_side((inputs, out_grad), "gx", 0, 1)
    gate_cols, up_cols = side_by_side((gate_weight, up_weight), "gz", 1, 0)
    down_cols = lax.all_gather(down_weight, "gz", axis=0, tiled=True)
    gate, upper, hidden_grad = partial_terms(rows_in, rows_grad, gate_cols, up_cols, down_cols)
    gate, upper, hidden_grad = side_by_side_2((gate, upper, hidden_grad), "gy", 0, 1)
    gate_grad, up_grad = local_grads(gate, upper, hidden_grad)
    gate_grad, up_grad = side_by_side((gate_grad, up_grad), "gy", 0, 1)
    partial_value = contract_last(gate_grad, gate_cols) + contract_last(up_grad, up_cols)
    summed = lax.psum_scatter(partial_value, "gx", scatter_dimension=0, tiled=True)
    return summed.astype(jnp.bfloat16)


def solution(mesh):
    return jax.shard_map(
        shards,
        mesh=mesh,
        in_specs=(
            P(("gx", "gz"), "gy"),
            P(("gx", "gz"), "gy"),
            P("gy", ("gx", "gz")),
            P("gy", ("gx", "gz")),
            P(("gx", "gz"), "gy"),
        ),
        out_specs=P(("gx", "gz"), "gy"),
        check_vma=False,
    )
```

profile of v0, /device:TPU:0, one launch (start us, length us, event | category | flops | bytes accessed | tf_op | source)
XLA Modules:
  0.0 562.6 jit_solution(5374275995693381164)
XLA Ops:
  6.5 2.1 pad_maximum_fusion.3
  8.7 0.0 all-gather.9.cloned.1.call-start
  8.7 0.7 all-gather.9.cloned.1.call-update
  9.4 0.0 all-gather.7.cloned.1.call-start
  9.5 3.8 pad_maximum_fusion.1
  13.4 0.0 reduce-scatter.3.cloned.1.call-start
  13.4 60.7 %all-gather.5.cloned.1.call-done = bf16[640,4096]{1,0:T(8,128)(2,1)} async-done(((bf16[80,4096]{1,0:T(8,128)(2,1)}), bf16[640,4096]{1,0:T(8,128)(2,1)}) %all-gather.5.cloned.1.call-update) | async-done | bytes 5242896 | tf_op jit(solution)/shard_map/all_gather | solution.py:10
  74.1 62.6 %all-gather.9.cloned.1.call-done = bf16[2048,2048]{1,0:T(8,128)(2,1)} async-done(((bf16[512,2048]{1,0:T(8,128)(2,1)}), bf16[2048,2048]{1,0:T(8,128)(2,1)}) %all-gather.9.cloned.1.call-update) | async-done | bytes 8388624 | tf_op jit(solution)/shard_map/all_gather | solution.py:48
  136.7 11.1 %fusion.13 = f32[640,2048]{1,0:T(8,128)} fusion(bf16[2048,2048]{1,0:T(8,128)(2,1)} %all-gather.9.cloned.1.call-done, bf16[640,4096]{1,0:T(8,128)(2,1)} %all-gather.5.cloned.1.call-done), kind=kOutput, calls=%fused_computation.13 | convolution fusion | flops 5368709120 | bytes 16252928 | tf_op jit(solution)/shard_map/dot_general | solution.py:24
  147.8 100.0 %all-gather.7.cloned.1.call-done = bf16[4096,2048]{1,0:T(8,128)(2,1)} async-done(((bf16[4096,512]{1,0:T(8,128)(2,1)}), bf16[4096,2048]{1,0:T(8,128)(2,1)}) %all-gather.7.cloned.1.call-update) | async-done | bytes 16777232 | tf_op jit(solution)/shard_map/all_gather | solution.py:10
  247.8 8.9 %fusion.2 = f32[640,2048]{1,0:T(8,128)S(1)} fusion(bf16[4096,2048]{1,0:T(8,128)(2,1)} %all-gather.7.cloned.1.call-done, bf16[640,4096]{1,0:T(8,128)(2,1)} %all-gather.5.cloned.1.call-done), kind=kOutput, calls=%fused_computation.3 | convolution fusion | flops 5368709120 | bytes 16252928 | tf_op jit(solution)/shard_map/dot_general | solution.py:31
  256.7 8.1 %fusion.6 = f32[640,2048]{1,0:T(8,128)S(1)} fusion(bf16[4096,2048]{1,0:T(8,128)(2,1)} %all-gather.7.cloned.1.call-done, bf16[640,4096]{1,0:T(8,128)(2,1)S(1)} %copy-done.1), kind=kOutput, calls=%fused_computation.7 | convolution fusion | flops 5368709120 | bytes 16252928 | tf_op jit(solution)/shard_map/dot_general | solution.py:30
  264.9 5.8 %pad_maximum_fusion = f32[640,6144]{1,0:T(8,128)} fusion(f32[640,2048]{1,0:T(8,128)S(1)} %bitcast.2, f32[640,2048]{1,0:T(8,128)S(1)} %fusion.2, f32[640,2048]{1,0:T(8,128)S(1)} %fusion.6), kind=kLoop, calls=%fused_computation | loop fusion | flops 7864320 | bytes 31457280 | tf_op jit(solution)/shard_map/concatenate | solution.py:15
  270.7 0.0 all-gather.11.cloned.1.call-start
  270.8 139.6 %reduce-scatter.3.cloned.1.call-done = f32[160,6144]{1,0:T(8,128)} async-done(((f32[640,6144]{1,0:T(8,128)}), f32[160,6144]{1,0:T(8,128)}) %reduce-scatter.3.cloned.1.call-update) | async-done | bytes 3932176 | tf_op jit(solution)/shard_map/reduce_scatter | solution.py:16
  410.4 2.8 fusion.19
  413.2 1.2 pad_maximum_fusion.2
  414.4 0.0 all-gather.11.cloned.1.call-update
  414.4 0.2 reduce-scatter.5.cloned.1.call-start
  414.6 56.6 %all-gather.11.cloned.1.call-done = bf16[640,4096]{1,0:T(8,128)(2,1)} async-done(((bf16[160,4096]{1,0:T(8,128)(2,1)}), bf16[640,4096]{1,0:T(8,128)(2,1)}) %all-gather.11.cloned.1.call-update) | async-done | bytes 5242896 | tf_op jit(solution)/shard_map/all_gather | solution.py:10
  471.2 9.0 %fusion = f32[640,2048]{1,0:T(8,128)S(1)} fusion(bf16[4096,2048]{1,0:T(8,128)(2,1)} %all-gather.7.cloned.1.call-done, bf16[640,4096]{1,0:T(8,128)(2,1)} %all-gather.11.cloned.1.call-done), kind=kOutput, calls=%fused_computation.1 | convolution fusion | flops 5368709120 | bytes 16252928 | tf_op jit(solution)/shard_map/dot_general | solution.py:24
  480.2 9.8 %fusion.8 = f32[640,2048]{1,0:T(8,128)} fusion(f32[640,2048]{1,0:T(8,128)S(1)} %fusion, bf16[4096,2048]{1,0:T(8,128)(2,1)} %all-gather.7.cloned.1.call-done, bf16[640,4096]{1,0:T(8,128)(2,1)S(1)} %copy-done.2), kind=kOutput, calls=%fused_computation.10 | convolution fusion | flops 5370019840 | bytes 21495808 | tf_op jit(solution)/shard_map/dot_general | solution.py:24
  490.1 63.8 %reduce-scatter.5.cloned.1.call-done = f32[80,2048]{1,0:T(8,128)} async-done(((f32[640,2048]{1,0:T(8,128)}), f32[80,2048]{1,0:T(8,128)}) %reduce-scatter.5.cloned.1.call-update) | async-done | bytes 655376 | tf_op jit(solution)/shard_map/reduce_scatter | solution.py:54
  553.9 1.8 convert_element_type.11
  (16 shorter events, 0.1 us)
Async XLA Ops:
  6.5 2.9 copy-start
  6.5 67.5 %all-gather.5.cloned.1.call-start = ((), (), s32[]{:S(2)}) async-start(), calls=%async_computation.2 | async-start | bytes 5898240 | tf_op jit(solution)/shard_map/all_gather | solution.py:10
  8.7 128.0 %all-gather.9.cloned.1.call-start = ((), (), s32[]{:S(2)}) async-start(), calls=%async_computation.4 | async-start | bytes 10485760 | tf_op jit(solution)/shard_map/all_gather | solution.py:48
  9.4 238.3 %all-gather.7.cloned.1.call-start = ((), (), s32[]{:S(2)}) async-start(), calls=%async_computation.3 | async-start | bytes 20971520 | tf_op jit(solution)/shard_map/all_gather | solution.py:10
  13.4 397.0 %reduce-scatter.3.cloned.1.call-start = ((), (), s32[]{:S(2)}) async-start(), calls=%async_computation.5 | async-start | bytes 19660800 | tf_op jit(solution)/shard_map/reduce_scatter | solution.py:16
  247.8 8.9 %copy-start.1 = (bf16[640,4096]{1,0:T(8,128)(2,1)S(1)}, bf16[640,4096]{1,0:T(8,128)(2,1)}, u32[]{:S(2)}) copy-start(bf16[640,4096]{1,0:T(8,128)(2,1)} %all-gather.5.cloned.1.call-done) | copy-start | bytes 15728644
  247.8 17.1 %slice-start = ((s8[5242880]{0:T(1024)(128)(4,1)}), s8[4194304]{0:T(1024)(128)(4,1)S(1)}, s32[]{:S(2)}) async-start(s8[5242880]{0:T(1024)(128)(4,1)} %bitcast.1), calls=%async_computation.8 | async-start | bytes 8388608
  256.7 8.1 %slice-start.1 = ((s8[5242880]{0:T(1024)(128)(4,1)}), s8[1048576]{0:T(1024)(128)(4,1)S(1)}, s32[]{:S(2)}) async-start(s8[5242880]{0:T(1024)(128)(4,1)} %bitcast.1), calls=%async_computation.9 | async-start | bytes 2097152
  270.7 200.5 %all-gather.11.cloned.1.call-start = ((), (), s32[]{:S(2)}) async-start(), calls=%async_computation.6 | async-start | bytes 6553600 | tf_op jit(solution)/shard_map/all_gather | solution.py:10
  414.4 139.5 %reduce-scatter.5.cloned.1.call-start = ((), (), s32[]{:S(2)}) async-start(), calls=%async_computation.7 | async-start | bytes 5898240 | tf_op jit(solution)/shard_map/reduce_scatter | solution.py:54
  471.2 9.0 %copy-start.2 = (bf16[640,4096]{1,0:T(8,128)(2,1)S(1)}, bf16[640,4096]{1,0:T(8,128)(2,1)}, u32[]{:S(2)}) copy-start(bf16[640,4096]{1,0:T(8,128)(2,1)} %all-gather.11.cloned.1.call-done) | copy-start | bytes 15728644
Sparse Core Ops, SparseCore 0:
  9.0 65.0 all-gather.4
  75.7 60.9 all-gather.8
  138.4 109.3 all-gather.6
  270.8 139.4 reduce-scatter.2
  414.5 56.6 all-gather.10
  490.2 63.6 reduce-scatter.4
where the time goes:
time: 563 us
  waiting for transfers between devices  484 us (86%)
  matrix products  47 us (8%)
  other arithmetic  17.7 us (3%)
  between operations  13.6 us (2%)
    all_gather x3, waiting for transfers between devices, side_by_side(): filled = lax.all_gather(both, axis, axis=dim, tiled=True)  217 us
    reduce_scatter x1, waiting for transfers between devices, side_by_side_2(): lax.psum_scatter(both, axis, scatter_dimension=dim, tiled=True)  140 us
    reduce_scatter x1, waiting for transfers between devices, shards(): lax.psum_scatter(partial_value, 'gx', scatter_dimension=0, tiled=True)  63.8 us
    all_gather x1, waiting for transfers between devices, shards(): down_cols = lax.all_gather(down_weight, 'gz', axis=0, tiled=True)  62.6 us
    dot_general x3, matrix products, contract_last(): lax.dot_general(left, right, (((1,), (1,)), ((), ())), preferred_element_...  29.9 us
  transfers between devices with their start and end apart: 6, of which 6 were waited for; matrix products, arithmetic and copies ran while one was open for 3% of the time, Pallas kernels for 0%

commit v1 on v0

v1 whole, which is shorter than its diff:
```python
import jax
import jax.numpy as jnp
from jax import lax
from jax.experimental import pallas as pl
from jax.experimental.pallas import tpu as pltpu
from jax.sharding import PartitionSpec as P

MESH = pl.DeviceIdType.MESH
F32 = jnp.float32
BF16 = jnp.bfloat16

ROWS = 80
WIDTH = 2048
HALF = WIDTH // 2
OWN = 512
Q = 256
PAIR = 2 * ROWS

GROUPS = ((0, 0), (1, 0), (1, 1), (3, 0), (3, 1), (2, 0), (2, 1), (0, 1))


def contract_last(left, right):
    return lax.dot_general(
        left, right, (((1,), (1,)), ((), ())), preferred_element_type=F32
    )


class Copies:
    def __init__(self, send_sems, recv_sems):
        self.send_sems, self.recv_sems = send_sems, recv_sems
        self.made, self.sent, self.landed = {}, [], set()

    def send(self, name, src, dst, device):
        k = len(self.made)
        copy = pltpu.make_async_remote_copy(
            src_ref=src,
            dst_ref=dst,
            send_sem=self.send_sems.at[k],
            recv_sem=self.recv_sems.at[k],
            device_id=device,
            device_id_type=MESH,
        )
        self.made[name] = copy
        self.sent.append(name)
        copy.start()

    def need(self, *names):
        for name in names:
            if name not in self.landed:
                self.landed.add(name)
                self.made[name].wait_recv()

    def free(self, *names):
        for name in names:
            if name in self.sent:
                self.sent.remove(name)
                self.made[name].wait_send()

    def finish(self):
        for name in list(self.made):
            self.need(name)
        self.free(*list(self.sent))


N_COPIES = 128
N_LOCAL = 7


def kernel(
    x_hbm, g_hbm, wg_hbm, wu_hbm, wd_hbm, out_ref,
    A, B, Wgu, Wd, S, O, ra, rb, H, sa, sb, xsa, xsb, xa, xb, zr,
    send_sems, recv_sems, local_sems,
):
    gx, y, gz = lax.axis_index("gx"), lax.axis_index("gy"), lax.axis_index("gz")
    x = lax.div(gz, 2) * 2 + lax.div(gx, 4)
    z = lax.rem(gx, 4)
    core = lax.rem(gz, 2)

    def device(dx=0, dy=0, dz=0):
        nx, ny, nz = (lax.rem(p + d + 4, 4) for p, d in ((x, dx), (y, dy), (z, dz)))
        return {
            "gx": lax.rem(nx, 2) * 4 + nz,
            "gy": ny,
            "gz": lax.div(nx, 2) * 2 + core,
        }

    partner = {"gx": gx, "gy": y, "gz": gz + 1 - 2 * core}
    xp, xm = device(dx=1), device(dx=-1)
    yp, ym = device(dy=1), device(dy=-1)
    zp, zm, zz = device(dz=1), device(dz=-1), device(dz=2)

    barrier = pltpu.get_barrier_semaphore()
    peers = (partner, xp, xm, yp, ym, zp, zm, zz)
    for peer in peers:
        pl.semaphore_signal(barrier, inc=1, device_id=peer, device_id_type=MESH)
    pl.semaphore_wait(barrier, len(peers))

    c = Copies(send_sems, recv_sems)
    L, R = pl.ds(0, HALF), pl.ds(HALF, HALF)

    c.send("Ax+", x_hbm, A.at[0, 3], xp)
    c.send("Ax-", x_hbm, A.at[0, 1], xm)
    c.send("Bz+", g_hbm, B.at[3, 0], zp)
    c.send("Bz-", g_hbm, B.at[1, 0], zm)
    locals_ = []

    def local(src, dst):
        copy = pltpu.make_async_copy(src, dst, local_sems.at[len(locals_)])
        copy.start()
        locals_.append(copy)

    local(x_hbm, A.at[0, 0])
    local(g_hbm, B.at[0, 0])
    blocks = []
    for j in range(2):
        at = pl.multiple_of((2 * core + j) * (2 * Q), 2 * Q)
        blocks.append((wg_hbm.at[:, pl.ds(j * Q, Q)], Wgu.at[:, pl.ds(at, Q)]))
        blocks.append((wu_hbm.at[:, pl.ds(j * Q, Q)], Wgu.at[:, pl.ds(at + Q, Q)]))
    blocks.append((wd_hbm, Wd.at[pl.ds(pl.multiple_of(core * OWN, OWN), OWN), :]))
    for k, (src, dst) in enumerate(blocks):
        c.send(f"w{k}", src, dst, partner)
        local(src, dst)
    c.send("Bx+0", g_hbm, B.at[0, 3], xp)
    c.send("Bx-0", g_hbm, B.at[0, 1], xm)
    c.send("Az+0", x_hbm, A.at[3, 0], zp)
    c.send("Az-0", x_hbm, A.at[1, 0], zm)

    def a_over_z(dx):
        c.send(f"Az+{dx}", A.at[0, dx], A.at[3, dx], zp)
        c.send(f"Az-{dx}", A.at[0, dx], A.at[1, dx], zm)

    def a_over_z_far(dx):
        c.need(f"Az+{dx}", f"Az-{dx}")
        c.send(f"Azf+{dx}", A.at[3, dx, :, L], A.at[2, dx, :, L], zp)
        c.send(f"Azf-{dx}", A.at[1, dx, :, R], A.at[2, dx, :, R], zm)

    def b_over_x(dz):
        c.send(f"Bx+{dz}", B.at[dz, 0], B.at[dz, 3], xp)
        c.send(f"Bx-{dz}", B.at[dz, 0], B.at[dz, 1], xm)

    def b_over_x_far(dz):
        c.need(f"Bx+{dz}", f"Bx-{dz}")
        c.send(f"Bxf+{dz}", B.at[dz, 3, :, L], B.at[dz, 2, :, L], xp)
        c.send(f"Bxf-{dz}", B.at[dz, 1, :, R], B.at[dz, 2, :, R], xm)

    def relay_0():
        c.need("Ax+", "Ax-")
        a_over_z(1)
        a_over_z(3)
        c.need("Bz+", "Bz-")
        b_over_x(1)
        c.send("Axf+", A.at[0, 3, :, L], A.at[0, 2, :, L], xp)
        c.send("Axf-", A.at[0, 1, :, R], A.at[0, 2, :, R], xm)
        c.send("Bzf+", B.at[3, 0, :, L], B.at[2, 0, :, L], zp)
        c.send("Bzf-", B.at[1, 0, :, R], B.at[2, 0, :, R], zm)

    def relay_1():
        b_over_x_far(1)
        b_over_x(3)
        c.need("Axf+", "Axf-")
        a_over_z(2)

    def relay_2():
        b_over_x_far(3)
        a_over_z_far(0)
        a_over_z_far(1)
        c.need("Bzf+", "Bzf-")
        b_over_x(2)

    def relay_3():
        a_over_z_far(3)
        a_over_z_far(2)
        b_over_x_far(0)
        b_over_x_far(2)

    relays = {0: relay_0, 1: relay_1, 2: relay_2, 3: relay_3}

    def need_tokens(dz, pair):
        if (dz, pair) == (0, 0):
            for copy in locals_:
                copy.wait()
            c.need(*(f"w{k}" for k in range(len(blocks))))
        for dx in (2 * pair, 2 * pair + 1):
            if dz == 0:
                names = {0: (), 1: ("Ax-",), 2: ("Axf+", "Axf-"), 3: ("Ax+",)}[dx]
            else:
                names = {1: (f"Az-{dx}",), 2: (f"Azf+{dx}", f"Azf-{dx}"), 3: (f"Az+{dx}",)}[dz]
            c.need(*names)
            if dx == 0:
                names = {0: (), 1: ("Bz-",), 2: ("Bzf+", "Bzf-"), 3: ("Bz+",)}[dz]
            else:
                names = {1: (f"Bx-{dz}",), 2: (f"Bxf+{dz}", f"Bxf-{dz}"), 3: (f"Bx+{dz}",)}[dx]
            c.need(*names)

    def quarter(k):
        return lax.rem(y + k, 4)

    def forward(g):
        dz, pair = GROUPS[g]
        need_tokens(dz, pair)

        @pl.loop(0, 4)
        def _(k):
            q = lax.rem(y + 2 + k, 4)
            rows_in = A[dz, 2 * pair : 2 * pair + 2].reshape(PAIR, WIDTH)
            w = Wgu[:, pl.ds(pl.multiple_of(q * 2 * Q, 2 * Q), 2 * Q)]
            S[g % 2, k, :, 0 : 2 * Q] = jnp.dot(rows_in, w, preferred_element_type=F32)
            rows_grad = B[dz, 2 * pair : 2 * pair + 2].reshape(PAIR, WIDTH)
            d = Wd[pl.ds(pl.multiple_of(q * Q, Q), Q), :]
            S[g % 2, k, :, 2 * Q : 3 * Q] = contract_last(rows_grad, d)

    def reduce_far(g):
        s = g % 2
        if g >= 2:
            c.free(f"ra+{g - 2}", f"ra-{g - 2}")
        sa[s] = S[s, 0].astype(BF16)
        c.send(f"ra+{g}", sa.at[s, pl.ds(0, ROWS)], ra.at[g, 0], yp)
        c.send(f"ra-{g}", sa.at[s, pl.ds(ROWS, ROWS)], ra.at[g, 1], ym)

    def reduce_near(g):
        s = g % 2
        if g >= 2:
            c.free(f"rb+{g - 2}", f"rb-{g - 2}")
        c.need(f"ra+{g}", f"ra-{g}")
        sb[s, 0, 0:ROWS] = (S[s, 3, 0:ROWS] + ra[g, 0].astype(F32)).astype(BF16)
        sb[s, 0, ROWS:PAIR] = S[s, 3, ROWS:PAIR].astype(BF16)
        c.send(f"rb+{g}", sb.at[s, 0], rb.at[g, 0], yp)
        sb[s, 1, 0:ROWS] = S[s, 1, 0:ROWS].astype(BF16)
        sb[s, 1, ROWS:PAIR] = (S[s, 1, ROWS:PAIR] + ra[g, 1].astype(F32)).astype(BF16)
        c.send(f"rb-{g}", sb.at[s, 1], rb.at[g, 1], ym)

    def grads(g):
        s = g % 2
        c.need(f"rb+{g}", f"rb-{g}")

        def total(at):
            cols = pl.ds(at, Q)
            return S[s, 2, :, cols] + rb[g, 0, :, cols].astype(F32) + rb[g, 1, :, cols].astype(F32)

        gate, upper, hidden_grad = total(0), total(Q), total(2 * Q)
        logistic = 1.0 / (1.0 + jnp.exp(-gate))
        scaled = hidden_grad * logistic
        at = pl.multiple_of(y * (2 * Q), 2 * Q)
        H[g, :, pl.ds(at, Q)] = (scaled * upper * (1.0 + gate * (1.0 - logistic))).astype(BF16)
        H[g, :, pl.ds(at + Q, Q)] = (scaled * gate).astype(BF16)
        own = H.at[g, :, pl.ds(at, 2 * Q)]
        c.send(f"ga+{g}", own, own, yp)
        c.send(f"ga-{g}", own, own, ym)

    def spread(g):
        c.need(f"ga+{g}", f"ga-{g}")
        at = pl.multiple_of(quarter(3) * (2 * Q), 2 * Q)
        part = H.at[g, :, pl.ds(at, Q)]
        c.send(f"gf+{g}", part, part, yp)
        at = pl.multiple_of(quarter(1) * (2 * Q), 2 * Q)
        part = H.at[g, :, pl.ds(at + Q, Q)]
        c.send(f"gf-{g}", part, part, ym)

    def backward(g):
        dz, pair = GROUPS[g]
        c.need(f"gf+{g}", f"gf-{g}")

        @pl.loop(0, 4)
        def _(n):
            at = pl.multiple_of(n * 512, 512)
            o = contract_last(H[g], Wgu[pl.ds(at, 512), :])
            O[dz, 2 * pair : 2 * pair + 2, :, pl.ds(at, 512)] = o.reshape(2, ROWS, 512)

    order = []

    def out_far(r):
        s = len(order) % 2
        order.append(r)
        if len(order) > 2:
            old = order[-3]
            c.free(f"xa+{old}", f"xa-{old}", f"xb+{old}", f"xb-{old}")
        xsa[s] = O[r, 2].astype(BF16)
        c.send(f"xa+{r}", xsa.at[s, :, L], xa.at[r, 0], xp)
        c.send(f"xa-{r}", xsa.at[s, :, R], xa.at[r, 1], xm)

    def out_near(r):
        s = order.index(r) % 2
        c.need(f"xa+{r}", f"xa-{r}")
        xsb[s, 0, :, 0:HALF] = (O[r, 1, :, 0:HALF] + xa[r, 0].astype(F32)).astype(BF16)
        xsb[s, 0, :, HALF:WIDTH] = O[r, 1, :, HALF:WIDTH].astype(BF16)
        c.send(f"xb+{r}", xsb.at[s, 0], xb.at[r, 0], xp)
        xsb[s, 1, :, 0:HALF] = O[r, 3, :, 0:HALF].astype(BF16)
        xsb[s, 1, :, HALF:WIDTH] = (O[r, 3, :, HALF:WIDTH] + xa[r, 1].astype(F32)).astype(BF16)
        c.send(f"xb-{r}", xsb.at[s, 1], xb.at[r, 1], xm)

    def out_sum(r):
        c.need(f"xb+{r}", f"xb-{r}")
        total = O[r, 0] + xb[r, 0].astype(F32) + xb[r, 1].astype(F32)
        if r == 0:
            c.need("z1", "z2", "z3")
            out_ref[...] = (total + zr[0] + zr[1] + zr[2]).astype(out_ref.dtype)
        else:
            O[r, 0] = total
            c.send(f"z{r}", O.at[r, 0], zr.at[r - 1], {1: zp, 2: zz, 3: zm}[r])

    relays[0]()
    forward(0)
    last = len(GROUPS) - 1
    finished = {g: dz for g, (dz, pair) in enumerate(GROUPS) if pair == 1}
    for t in range(last + 2):
        if t <= last:
            reduce_far(t)
        if t >= 1:
            grads(t - 1)
        if t >= 2:
            backward(t - 2)
            if t - 2 in finished:
                out_far(finished[t - 2])
        if t <= last:
            reduce_near(t)
        if t - 3 in finished:
            out_sum(finished[t - 3])
        if t + 1 <= last:
            if t + 1 in relays:
                relays[t + 1]()
            forward(t + 1)
        if t >= 1:
            spread(t - 1)
        if t - 2 in finished:
            out_near(finished[t - 2])
    backward(last)
    out_far(finished[last])
    out_sum(finished[last - 1])
    out_near(finished[last])
    out_sum(finished[last])
    c.finish()


def shards(inputs, out_grad, gate_weight, up_weight, down_weight):
    groups = len(GROUPS)
    return pl.pallas_call(
        kernel,
        out_shape=jax.ShapeDtypeStruct((ROWS, WIDTH), BF16),
        in_specs=[pl.BlockSpec(memory_space=pl.ANY)] * 5,
        out_specs=pl.BlockSpec(memory_space=pltpu.VMEM),
        scratch_shapes=[
            pltpu.VMEM((4, 4, ROWS, WIDTH), BF16),
            pltpu.VMEM((4, 4, ROWS, WIDTH), BF16),
            pltpu.VMEM((WIDTH, 8 * Q), BF16),
            pltpu.VMEM((4 * Q, WIDTH), BF16),
            pltpu.VMEM((2, 4, PAIR, 3 * Q), F32),
            pltpu.VMEM((4, 4, ROWS, WIDTH), F32),
            pltpu.VMEM((groups, 2, ROWS, 3 * Q), BF16),
            pltpu.VMEM((groups, 2, PAIR, 3 * Q), BF16),
            pltpu.VMEM((groups, PAIR, 8 * Q), BF16),
            pltpu.VMEM((2, PAIR, 3 * Q), BF16),
            pltpu.VMEM((2, 2, PAIR, 3 * Q), BF16),
            pltpu.VMEM((2, ROWS, WIDTH), BF16),
            pltpu.VMEM((2, 2, ROWS, WIDTH), BF16),
            pltpu.VMEM((4, 2, ROWS, HALF), BF16),
            pltpu.VMEM((4, 2, ROWS, WIDTH), BF16),
            pltpu.VMEM((3, ROWS, WIDTH), F32),
            pltpu.SemaphoreType.DMA((N_COPIES,)),
            pltpu.SemaphoreType.DMA((N_COPIES,)),
            pltpu.SemaphoreType.DMA((N_LOCAL,)),
        ],
        compiler_params=pltpu.CompilerParams(
            collective_id=0, has_side_effects=True, vmem_limit_bytes=66_500_000
        ),
        name="swiglu_back",
    )(inputs, out_grad, gate_weight, up_weight, down_weight)


def solution(mesh):
    return jax.shard_map(
        shards,
        mesh=mesh,
        in_specs=(
            P(("gx", "gz"), "gy"),
            P(("gx", "gz"), "gy"),
            P("gy", ("gx", "gz")),
            P("gy", ("gx", "gz")),
            P(("gx", "gz"), "gy"),
        ),
        out_specs=P(("gx", "gz"), "gy"),
        check_vma=False,
    )
```

time: 563 us -> 171 us (0.30)
  waiting for transfers between devices: 484 us -> 0 us
  Pallas kernels: 0 us -> 169 us
  matrix products: 47 us -> 0 us
  other arithmetic: 17.7 us -> 0 us
  between operations: 13.6 us -> 0.01 us
    all_gather x4 -> x0, waiting for transfers between devices: 280 us -> none  [the longest x3 217 us: side_by_side(): filled = lax.all_gather(both, axis, axis=dim, tiled=True)]
    reduce_scatter x2 -> x0, waiting for transfers between devices: 203 us -> none  [the longest x1 140 us: side_by_side_2(): lax.psum_scatter(both, axis, scatter_dimension=dim, tiled=True)]
    pallas_call x0 -> x1, Pallas kernels: none -> 169 us  [shards(): pl.pallas_call(kernel, out_shape=jax.ShapeDtypeStruct((ROWS, WIDTH), BF16...]
    dot_general x5 -> x0, matrix products: 47 us -> none  [the longest x3 29.9 us: contract_last(): lax.dot_general(left, right, (((1,), (1,)), ((), ())), preferred_element_...]
    concatenate x4 -> x0, other arithmetic: 13 us -> none  [the longest x3 7.16 us: side_by_side(): both = jnp.concatenate(arrays, axis=along)]
  transfers between devices with their start and end apart: 6 -> 0, of which waited for: 6 -> 0; matrix products, arithmetic and copies ran while one was open for 3% -> 0% of each run, Pallas kernels for 0% -> 0%
where the time goes in v1:
time: 171 us
  Pallas kernels  169 us (99%)
  local copies, waits for them, and re-layouts  1.72 us (1%)
    pallas_call x1, Pallas kernels, shards(): pl.pallas_call(kernel, out_shape=jax.ShapeDtypeStruct((ROWS, WIDTH), BF16...  169 us

profile of v1, /device:TPU:0, one launch (start us, length us, event | category | flops | bytes accessed | tf_op | source)
XLA Modules:
  0.0 170.9 jit_solution(13217153644295343579)
XLA Ops:
  0.0 169.2 %swiglu_back.1 = bf16[80,2048]{1,0:T(8,128)(2,1)} custom-call(bf16[80,2048]{1,0:T(8,128)(2,1)} %x_hbm.1, bf16[80,2048]{1,0:T(8,128)(2,1)} %g_hbm.1, bf16[2048,512]{1,0:T(8,128)(2,1)} %wg_hbm.1, bf16[2048,512]{1,0:T(8,128)(2,1)} %wu_hbm.1, bf16[512,2048]{1,0:T(8,128)(2,1)} %wd_hbm.1), custom_call_target="tpu_custom_call" | custom-call | tf_op jit(solution)/shard_map/swiglu_back/pallas_call | solution.py:336
  169.2 1.7 %copy.7 = bf16[80,2048]{1,0:T(8,128)(2,1)} copy(bf16[80,2048]{1,0:T(8,128)(2,1)} %swiglu_back.1) | data formatting | bytes 655360

commit v2 on v1

v2 whole, which is shorter than its diff:
```python
import jax
import jax.numpy as jnp
from jax import lax
from jax.experimental import pallas as pl
from jax.experimental.pallas import tpu as pltpu
from jax.sharding import PartitionSpec as P

MESH = pl.DeviceIdType.MESH
F32 = jnp.float32
BF16 = jnp.bfloat16

ROWS = 80
WIDTH = 2048
HALF = WIDTH // 2
OWN = 512
Q = 256
CUT = 3 * Q // 2

GROUPS = (
    ((0, 0, 0, 64),),
    ((1, 0, 0, 80), (3, 0, 0, 80)),
    ((1, 1, 0, 80), (1, 3, 0, 80)),
    ((3, 1, 0, 80), (3, 3, 0, 80)),
    ((1, 2, 0, 80), (3, 2, 0, 80)),
    ((2, 2, 0, 80), (2, 1, 0, 80)),
    ((2, 3, 0, 80), (2, 0, 0, 80)),
    ((0, 2, 0, 80), (0, 1, 0, 80)),
    ((0, 3, 0, 80), (0, 0, 64, 16)),
)
SIZES = tuple(sum(rows for *_, rows in group) for group in GROUPS)
STARTS = tuple(sum(SIZES[:g]) for g in range(len(SIZES)))
TOP = max(SIZES)
ALL = sum(SIZES)


def contract_last(left, right):
    return lax.dot_general(
        left, right, (((1,), (1,)), ((), ())), preferred_element_type=F32
    )


class Copies:
    def __init__(self, send_sems, recv_sems):
        self.send_sems, self.recv_sems = send_sems, recv_sems
        self.made, self.sent, self.landed = {}, [], set()

    def send(self, name, src, dst, device):
        k = len(self.made)
        copy = pltpu.make_async_remote_copy(
            src_ref=src,
            dst_ref=dst,
            send_sem=self.send_sems.at[k],
            recv_sem=self.recv_sems.at[k],
            device_id=device,
            device_id_type=MESH,
        )
        self.made[name] = copy
        self.sent.append(name)
        copy.start()

    def need(self, *names):
        for name in names:
            if name not in self.landed:
                self.landed.add(name)
                self.made[name].wait_recv()

    def free(self, *names):
        for name in names:
            if name in self.sent:
                self.sent.remove(name)
                self.made[name].wait_send()

    def finish(self):
        for name in list(self.made):
            self.need(name)
        self.free(*list(self.sent))


N_COPIES = 160
N_LOCAL = 7


def kernel(
    x_hbm, g_hbm, wg_hbm, wu_hbm, wd_hbm, out_ref,
    A, B, Wgu, Wd, S, O, ra, rb, H, sa, sb, xsa, xsb, xa, xb, zr,
    send_sems, recv_sems, local_sems,
):
    gx, y, gz = lax.axis_index("gx"), lax.axis_index("gy"), lax.axis_index("gz")
    x = lax.div(gz, 2) * 2 + lax.div(gx, 4)
    z = lax.rem(gx, 4)
    core = lax.rem(gz, 2)

    def device(dx=0, dy=0, dz=0):
        nx, ny, nz = (lax.rem(p + d + 4, 4) for p, d in ((x, dx), (y, dy), (z, dz)))
        return {
            "gx": lax.rem(nx, 2) * 4 + nz,
            "gy": ny,
            "gz": lax.div(nx, 2) * 2 + core,
        }

    partner = {"gx": gx, "gy": y, "gz": gz + 1 - 2 * core}
    xp, xm = device(dx=1), device(dx=-1)
    yp, ym = device(dy=1), device(dy=-1)
    zp, zm, zz = device(dz=1), device(dz=-1), device(dz=2)

    barrier = pltpu.get_barrier_semaphore()
    peers = (partner, xp, xm, yp, ym, zp, zm, zz)
    for peer in peers:
        pl.semaphore_signal(barrier, inc=1, device_id=peer, device_id_type=MESH)
    pl.semaphore_wait(barrier, len(peers))

    c = Copies(send_sems, recv_sems)
    L, R = pl.ds(0, HALF), pl.ds(HALF, HALF)

    c.send("Ax+", x_hbm, A.at[0, 3], xp)
    c.send("Ax-", x_hbm, A.at[0, 1], xm)
    c.send("Bz+", g_hbm, B.at[3, 0], zp)
    c.send("Bz-", g_hbm, B.at[1, 0], zm)
    c.send("Az+0", x_hbm, A.at[3, 0], zp)
    c.send("Az-0", x_hbm, A.at[1, 0], zm)
    locals_ = []

    def local(src, dst):
        copy = pltpu.make_async_copy(src, dst, local_sems.at[len(locals_)])
        copy.start()
        locals_.append(copy)

    local(x_hbm, A.at[0, 0])
    local(g_hbm, B.at[0, 0])
    blocks = []
    for j in range(2):
        at = pl.multiple_of((2 * core + j) * (2 * Q), 2 * Q)
        blocks.append((wg_hbm.at[:, pl.ds(j * Q, Q)], Wgu.at[:, pl.ds(at, Q)]))
        blocks.append((wu_hbm.at[:, pl.ds(j * Q, Q)], Wgu.at[:, pl.ds(at + Q, Q)]))
    blocks.append((wd_hbm, Wd.at[pl.ds(pl.multiple_of(core * OWN, OWN), OWN), :]))
    for k, (src, dst) in enumerate(blocks):
        c.send(f"w{k}", src, dst, partner)
        local(src, dst)

    def a_over_z(dx):
        c.send(f"Az+{dx}", A.at[0, dx], A.at[3, dx], zp)
        c.send(f"Az-{dx}", A.at[0, dx], A.at[1, dx], zm)

    def a_over_z_far(dx):
        c.need(f"Az+{dx}", f"Az-{dx}")
        c.send(f"Azf+{dx}", A.at[3, dx, :, L], A.at[2, dx, :, L], zp)
        c.send(f"Azf-{dx}", A.at[1, dx, :, R], A.at[2, dx, :, R], zm)

    def b_over_x(dz):
        c.send(f"Bx+{dz}", B.at[dz, 0], B.at[dz, 3], xp)
        c.send(f"Bx-{dz}", B.at[dz, 0], B.at[dz, 1], xm)

    def b_over_x_far(dz):
        c.need(f"Bx+{dz}", f"Bx-{dz}")
        c.send(f"Bxf+{dz}", B.at[dz, 3, :, L], B.at[dz, 2, :, L], xp)
        c.send(f"Bxf-{dz}", B.at[dz, 1, :, R], B.at[dz, 2, :, R], xm)

    def relay_0():
        c.need("Ax+", "Ax-")
        c.send("Axf+", A.at[0, 3, :, L], A.at[0, 2, :, L], xp)
        c.send("Axf-", A.at[0, 1, :, R], A.at[0, 2, :, R], xm)
        a_over_z(1)
        a_over_z(3)
        c.need("Bz+", "Bz-")
        b_over_x(1)
        b_over_x(3)
        c.send("Bzf+", B.at[3, 0, :, L], B.at[2, 0, :, L], zp)
        c.send("Bzf-", B.at[1, 0, :, R], B.at[2, 0, :, R], zm)

    def relay_2():
        c.need("Axf+", "Axf-")
        a_over_z(2)
        b_over_x_far(1)
        b_over_x_far(3)

    def relay_3():
        a_over_z_far(0)
        a_over_z_far(1)
        a_over_z_far(3)
        c.need("Bzf+", "Bzf-")
        b_over_x(2)

    def relay_4():
        a_over_z_far(2)
        b_over_x_far(2)
        b_over_x(0)

    def relay_5():
        b_over_x_far(0)

    relays = {0: relay_0, 2: relay_2, 3: relay_3, 4: relay_4, 5: relay_5}

    def need_tokens(g):
        if g == 0:
            for copy in locals_:
                copy.wait()
            c.need(*(f"w{k}" for k in range(len(blocks))))
        for dz, dx, *_ in GROUPS[g]:
            if dz == 0:
                c.need(*{0: (), 1: ("Ax-",), 2: ("Axf+", "Axf-"), 3: ("Ax+",)}[dx])
            else:
                c.need(*{1: (f"Az-{dx}",), 2: (f"Azf+{dx}", f"Azf-{dx}"), 3: (f"Az+{dx}",)}[dz])
            if dx == 0:
                c.need(*{0: (), 1: ("Bz-",), 2: ("Bzf+", "Bzf-"), 3: ("Bz+",)}[dz])
            else:
                c.need(*{1: (f"Bx-{dz}",), 2: (f"Bxf+{dz}", f"Bxf-{dz}"), 3: (f"Bx+{dz}",)}[dx])

    def rows_of(ref, g):
        parts = [ref[dz, dx, first : first + rows] for dz, dx, first, rows in GROUPS[g]]
        return parts[0] if len(parts) == 1 else jnp.concatenate(parts, axis=0)

    def quarter(k):
        return lax.rem(y + k, 4)

    def forward(g):
        m = SIZES[g]
        need_tokens(g)

        @pl.loop(0, 4)
        def _(k):
            q = lax.rem(y + 2 + k, 4)
            w = Wgu[:, pl.ds(pl.multiple_of(q * 2 * Q, 2 * Q), 2 * Q)]
            S[g % 2, k, 0:m, 0 : 2 * Q] = jnp.dot(rows_of(A, g), w, preferred_element_type=F32)
            d = Wd[pl.ds(pl.multiple_of(q * Q, Q), Q), :]
            S[g % 2, k, 0:m, 2 * Q : 3 * Q] = contract_last(rows_of(B, g), d)

    def reduce_far(g):
        s, m = g % 2, SIZES[g]
        at = pl.ds(STARTS[g], m)
        if g >= 2:
            c.free(f"ra+{g - 2}", f"ra-{g - 2}")
        sa[s, 0:m] = S[s, 0, 0:m].astype(BF16)
        c.send(f"ra+{g}", sa.at[s, pl.ds(0, m), pl.ds(0, CUT)], ra.at[0, at], yp)
        c.send(f"ra-{g}", sa.at[s, pl.ds(0, m), pl.ds(CUT, CUT)], ra.at[1, at], ym)

    def reduce_near(g):
        s, m = g % 2, SIZES[g]
        at = slice(STARTS[g], STARTS[g] + m)
        if g >= 2:
            c.free(f"rb+{g - 2}", f"rb-{g - 2}")
        c.need(f"ra+{g}", f"ra-{g}")
        sb[s, 0, 0:m, 0:CUT] = (S[s, 3, 0:m, 0:CUT] + ra[0, at].astype(F32)).astype(BF16)
        sb[s, 0, 0:m, CUT:] = S[s, 3, 0:m, CUT:].astype(BF16)
        c.send(f"rb+{g}", sb.at[s, 0, pl.ds(0, m)], rb.at[0, pl.ds(STARTS[g], m)], yp)
        sb[s, 1, 0:m, 0:CUT] = S[s, 1, 0:m, 0:CUT].astype(BF16)
        sb[s, 1, 0:m, CUT:] = (S[s, 1, 0:m, CUT:] + ra[1, at].astype(F32)).astype(BF16)
        c.send(f"rb-{g}", sb.at[s, 1, pl.ds(0, m)], rb.at[1, pl.ds(STARTS[g], m)], ym)

    def grads(g):
        s, m = g % 2, SIZES[g]
        rows = pl.ds(STARTS[g], m)
        c.need(f"rb+{g}", f"rb-{g}")

        def total(at):
            cols = pl.ds(at, Q)
            return S[s, 2, 0:m, cols] + rb[0, rows, cols].astype(F32) + rb[1, rows, cols].astype(F32)

        gate, upper, hidden_grad = total(0), total(Q), total(2 * Q)
        logistic = 1.0 / (1.0 + jnp.exp(-gate))
        scaled = hidden_grad * logistic
        at = pl.multiple_of(y * (2 * Q), 2 * Q)
        H[rows, pl.ds(at, Q)] = (scaled * upper * (1.0 + gate * (1.0 - logistic))).astype(BF16)
        H[rows, pl.ds(at + Q, Q)] = (scaled * gate).astype(BF16)
        own = H.at[rows, pl.ds(at, 2 * Q)]
        c.send(f"ga+{g}", own, own, yp)
        c.send(f"ga-{g}", own, own, ym)

    def spread(g):
        rows = pl.ds(STARTS[g], SIZES[g])
        c.need(f"ga+{g}", f"ga-{g}")
        at = pl.multiple_of(quarter(3) * (2 * Q), 2 * Q)
        part = H.at[rows, pl.ds(at, Q)]
        c.send(f"gf+{g}", part, part, yp)
        at = pl.multiple_of(quarter(1) * (2 * Q), 2 * Q)
        part = H.at[rows, pl.ds(at + Q, Q)]
        c.send(f"gf-{g}", part, part, ym)

    def backward(g):
        c.need(f"gf+{g}", f"gf-{g}")

        @pl.loop(0, 4)
        def _(n):
            cols = pl.ds(pl.multiple_of(n * 512, 512), 512)
            o = contract_last(H[STARTS[g] : STARTS[g] + SIZES[g]], Wgu[cols, :])
            done = 0
            for dz, dx, first, rows in GROUPS[g]:
                O[dz, dx, first : first + rows, cols] = o[done : done + rows]
                done += rows

    def out_far(r):
        xsa[r] = O[r, 2].astype(BF16)
        c.send(f"xa+{r}", xsa.at[r, :, L], xa.at[r, 0], xp)
        c.send(f"xa-{r}", xsa.at[r, :, R], xa.at[r, 1], xm)

    def out_plus(r):
        c.need(f"xa+{r}")
        xsb[r, 0, :, 0:HALF] = (O[r, 1, :, 0:HALF] + xa[r, 0].astype(F32)).astype(BF16)
        xsb[r, 0, :, HALF:WIDTH] = O[r, 1, :, HALF:WIDTH].astype(BF16)
        c.send(f"xb+{r}", xsb.at[r, 0], xb.at[r, 0], xp)

    def out_minus(r):
        c.need(f"xa-{r}")
        xsb[r, 1, :, 0:HALF] = O[r, 3, :, 0:HALF].astype(BF16)
        xsb[r, 1, :, HALF:WIDTH] = (O[r, 3, :, HALF:WIDTH] + xa[r, 1].astype(F32)).astype(BF16)
        c.send(f"xb-{r}", xsb.at[r, 1], xb.at[r, 1], xm)

    def out_sum(r):
        c.need(f"xb+{r}", f"xb-{r}")
        total = O[r, 0] + xb[r, 0].astype(F32) + xb[r, 1].astype(F32)
        if r == 0:
            c.need("z1", "z2", "z3")
            out_ref[...] = (total + zr[0] + zr[1] + zr[2]).astype(out_ref.dtype)
        else:
            O[r, 0] = total
            c.send(f"z{r}", O.at[r, 0], zr.at[r - 1], {1: zp, 2: zz, 3: zm}[r])

    after = {4: ((out_far, 1), (out_far, 3)), 5: ((out_far, 2),), 7: ((out_far, 0),)}
    later = {
        4: ((out_plus, 1), (out_minus, 1), (out_plus, 3), (out_minus, 3)),
        5: ((out_sum, 1), (out_sum, 3), (out_plus, 2)),
        6: ((out_minus, 2),),
    }

    def run(events):
        for event, r in events:
            event(r)

    relays[0]()
    forward(0)
    last = len(GROUPS) - 1
    for t in range(last + 2):
        if t <= last:
            reduce_far(t)
        if t >= 1:
            grads(t - 1)
        if t >= 2:
            backward(t - 2)
            run(after.get(t - 2, ()))
        if t <= last:
            reduce_near(t)
        if t + 1 <= last:
            if t + 1 in relays:
                relays[t + 1]()
            forward(t + 1)
        if t >= 1:
            spread(t - 1)
        run(later.get(t - 2, ()))
    out_sum(2)
    backward(last)
    out_minus(0)
    out_plus(0)
    out_sum(0)
    c.finish()


def shards(inputs, out_grad, gate_weight, up_weight, down_weight):
    return pl.pallas_call(
        kernel,
        out_shape=jax.ShapeDtypeStruct((ROWS, WIDTH), BF16),
        in_specs=[pl.BlockSpec(memory_space=pl.ANY)] * 5,
        out_specs=pl.BlockSpec(memory_space=pltpu.VMEM),
        scratch_shapes=[
            pltpu.VMEM((4, 4, ROWS, WIDTH), BF16),
            pltpu.VMEM((4, 4, ROWS, WIDTH), BF16),
            pltpu.VMEM((WIDTH, 8 * Q), BF16),
            pltpu.VMEM((4 * Q, WIDTH), BF16),
            pltpu.VMEM((2, 4, TOP, 3 * Q), F32),
            pltpu.VMEM((4, 4, ROWS, WIDTH), F32),
            pltpu.VMEM((2, ALL, CUT), BF16),
            pltpu.VMEM((2, ALL, 3 * Q), BF16),
            pltpu.VMEM((ALL, 8 * Q), BF16),
            pltpu.VMEM((2, TOP, 3 * Q), BF16),
            pltpu.VMEM((2, 2, TOP, 3 * Q), BF16),
            pltpu.VMEM((4, ROWS, WIDTH), BF16),
            pltpu.VMEM((4, 2, ROWS, WIDTH), BF16),
            pltpu.VMEM((4, 2, ROWS, HALF), BF16),
            pltpu.VMEM((4, 2, ROWS, WIDTH), BF16),
            pltpu.VMEM((3, ROWS, WIDTH), F32),
            pltpu.SemaphoreType.DMA((N_COPIES,)),
            pltpu.SemaphoreType.DMA((N_COPIES,)),
            pltpu.SemaphoreType.DMA((N_LOCAL,)),
        ],
        compiler_params=pltpu.CompilerParams(
            collective_id=0, has_side_effects=True, vmem_limit_bytes=66_500_000
        ),
        name="swiglu_back",
    )(inputs, out_grad, gate_weight, up_weight, down_weight)


def solution(mesh):
    return jax.shard_map(
        shards,
        mesh=mesh,
        in_specs=(
            P(("gx", "gz"), "gy"),
            P(("gx", "gz"), "gy"),
            P("gy", ("gx", "gz")),
            P("gy", ("gx", "gz")),
            P(("gx", "gz"), "gy"),
        ),
        out_specs=P(("gx", "gz"), "gy"),
        check_vma=False,
    )
```

time: 171 us -> 158 us (0.924)
  Pallas kernels: 169 us -> 156 us
    pallas_call x1, Pallas kernels: 169 us -> 156 us  [shards(): pl.pallas_call(kernel, out_shape=jax.ShapeDtypeStruct((ROWS, WIDTH), BF16...]
where the time goes in v2:
time: 158 us
  Pallas kernels  156 us (99%)
  local copies, waits for them, and re-layouts  1.72 us (1%)
    pallas_call x1, Pallas kernels, shards(): pl.pallas_call(kernel, out_shape=jax.ShapeDtypeStruct((ROWS, WIDTH), BF16...  156 us

profile of v2, /device:TPU:0, one launch (start us, length us, event | category | flops | bytes accessed | tf_op | source)
XLA Modules:
  0.0 158.2 jit_solution(16606407621554560842)
XLA Ops:
  0.0 156.4 %swiglu_back.1 = bf16[80,2048]{1,0:T(8,128)(2,1)} custom-call(bf16[80,2048]{1,0:T(8,128)(2,1)} %x_hbm.1, bf16[80,2048]{1,0:T(8,128)(2,1)} %g_hbm.1, bf16[2048,512]{1,0:T(8,128)(2,1)} %wg_hbm.1, bf16[2048,512]{1,0:T(8,128)(2,1)} %wu_hbm.1, bf16[512,2048]{1,0:T(8,128)(2,1)} %wd_hbm.1), custom_call_target="tpu_custom_call" | custom-call | tf_op jit(solution)/shard_map/swiglu_back/pallas_call | solution.py:357
  156.4 1.7 %copy.7 = bf16[80,2048]{1,0:T(8,128)(2,1)} copy(bf16[80,2048]{1,0:T(8,128)(2,1)} %swiglu_back.1) | data formatting | bytes 655360
